TPU v7x, 32 devices: a whole 2x2x4 slice. The times are simulated.
32 devices in a mesh: row: 8 (over y, x, core), col: 4 (over z).
Axes of the slice: x: 2, y: 2, z: 4, core: 2. Of those that a mesh axis runs over, the one named last changes fastest.
Arguments:
- features: bfloat16 [65536, 256], P(('row', 'col')), may hold values from -6 to 6
- tiles: bfloat16 [8, 4, 768, 128, 128], P('row', 'col'), as said below
- tile_rows: int32 [8, 4, 768], P('row', 'col'), may hold values from 0 to 63
- tile_cols: int32 [8, 4, 768], P('row', 'col'), may hold values from 0 to 127
- valid: int32 [8, 4, 768], P('row', 'col'), may hold values from 0 to 1, as said below
- weight: bfloat16 [256, 256], replicated, may hold values from -0.375 to 0.375
- bias: float32 [256], replicated, may hold values from -3 to 3
Outputs:
- hidden: bfloat16 [65536, 256], P(('row', 'col'))
Inputs may be any that keep to these rules, and one draw needn't show every extreme that they name: Each cell holds between 96 and 384 valid slots at any positions; in every draw some cell has exactly 384 valid slots. `tiles`: tile entries are non-negative.
All inputs are finite; a program needn't handle non-finite values.
Results may differ from a plain program's by a relative error of at most 0.0039.
Values may be sent and summed in bfloat16 or wider, within the bound.
A program may use at most 256 MiB of HBM per device.

v0:
```python
import jax
import jax.numpy as jnp
from jax import lax
from jax.sharding import PartitionSpec as P


def on_device(features, tiles, tile_rows, tile_cols, valid, weight, bias):
    sub_rows = features.shape[0]
    width = features.shape[1]
    tile_size = tiles.shape[3]
    slot_count = tiles.shape[2]
    block_size = min(slot_count, 128)
    col_count = lax.axis_size("col")
    row_tiles = sub_rows * col_count // tile_size
    panel = lax.all_gather(features, "row", axis=0, tiled=True)
    panel_tiles = panel.reshape(-1, tile_size, width)
    cell_tiles = tiles[0, 0]
    cell_rows = tile_rows[0, 0]
    cell_cols = tile_cols[0, 0]
    cell_valid = valid[0, 0]
    start_sum = jnp.zeros((row_tiles, tile_size, width), jnp.float32)

    def add_block(partial_sum, tile_block, row_block, col_block, flag_block):
        chosen = panel_tiles[col_block]
        products = jnp.einsum(
            "bij,bjf->bif", tile_block, chosen, preferred_element_type=jnp.float32
        )
        products = products * flag_block.astype(jnp.float32)[:, None, None]
        return partial_sum.at[row_block].add(products)

    ordering = jnp.argsort(1 - cell_valid, stable=True)
    live_count = jnp.sum(cell_valid)
    turns = (live_count + block_size - 1) // block_size

    def loop_step(turn, partial_sum):
        picked = lax.dynamic_slice_in_dim(ordering, turn * block_size, block_size)
        return add_block(
            partial_sum,
            cell_tiles[picked],
            cell_rows[picked],
            cell_cols[picked],
            cell_valid[picked],
        )

    partial_sum = lax.fori_loop(0, turns, loop_step, start_sum)
    partial_rows = partial_sum.reshape(row_tiles * tile_size, width)
    summed = lax.psum_scatter(partial_rows, "col", scatter_dimension=0, tiled=True)
    aggregated = summed.astype(jnp.bfloat16)
    mixed = jnp.dot(aggregated, weight, preferred_element_type=jnp.float32) + bias
    return jnp.maximum(mixed, 0.0).astype(jnp.bfloat16)


def solution(mesh):
    return jax.shard_map(
        on_device,
        mesh=mesh,
        in_specs=(
            P(("row", "col"), None),
            P("row", "col", None, None, None),
            P("row", "col", None),
            P("row", "col", None),
            P("row", "col", None),
            P(),
            P(),
        ),
        out_specs=P(("row", "col"), None),
        check_vma=False,
    )
```

profile of v0, /device:TPU:16, one launch (start us, length us, event | category | flops | bytes accessed | tf_op | source)
XLA Modules:
  0.0 450.0 jit_solution(15204184834748256117)
XLA Ops:
  6.5 0.0 copy-start
  6.5 0.0 all-gather.2.cloned.1.call-start
  6.5 0.7 all-gather.2.cloned.1.call-update
  7.3 0.0 reduce-scatter.2.cloned.1.call-start
  7.3 1.3 fusion.5
  9.3 0.7 reduce.2
  10.0 0.7 reduce.3
  10.7 4.4 sort.17
  15.1 49.5 %all-gather.2.cloned.1.call-done = bf16[16384,256]{1,0:T(8,128)(2,1)} async-done(((bf16[2048,256]{1,0:T(8,128)(2,1)}), bf16[16384,256]{1,0:T(8,128)(2,1)}) %all-gather.2.cloned.1.call-update) | async-done | bytes 8388624 | tf_op jit(solution)/shard_map/all_gather | solution.py:15
  64.6 4.2 broadcast_in_dim.4
  68.8 150.0 %while.10 = (s32[]{:T(128)}, f32[64,128,256]{2,1,0:T(8,128)}, s32[]{:T(128)}, s32[768]{0:T(1024)S(1)}, s32[768]{0:T(1024)S(1)}, /*index=5*/bf16[768,128,128]{2,1...) while((s32[]{:T(128)}, f32[64,128,256]{2,1,0:T(8,128)}, ...), condition=%wide.region_4.5_spmd, body=%wide.region_2.4_spmd.sunk | while | flops 1082133760 | bytes 104877744 | solution.py:45
  68.8 0.1 compare_select_fusion.4
  68.9 1.0 gather_fusion.4
  69.9 1.0 gather_fusion.2
  70.9 1.0 gather_fusion
  71.9 11.2 %gather_fusion.1 = bf16[128,128,128]{2,1,0:T(8,128)(2,1)} fusion(bf16[768,128,128]{2,1,0:T(8,128)(2,1)} %get-tuple-element.163, s32[1024]{0:T(1024)S(1)} %pad_clamp_fusion.4), kind=kCustom, calls=%fused_computation.1.clone.1 | custom fusion | bytes 8389120 | tf_op jit(solution)/shard_map/while/body/gather | solution.py:39
  83.0 9.9 %gather_fusion.3 = bf16[128,128,256]{2,1,0:T(8,128)(2,1)} fusion(bf16[128,128,256]{2,1,0:T(8,128)(2,1)} %get-tuple-element.165, s32[1024]{0:T(1024)S(1)} %pad_clamp_fusion.5), kind=kCustom, calls=%fused_computation.3.clone.1 | custom fusion | bytes 16777728 | tf_op jit(solution)/shard_map/while/body/gather | solution.py:24
  93.0 12.7 %convolution_multiply_fusion.2 = f32[128,128,256]{2,1,0:T(8,128)} fusion(bf16[128,128,128]{2,1,0:T(8,128)(2,1)} %gather_fusion.1, bf16[128,128,256]{2,1,0:T(8,128)(2,1)} %gather_fusion.3, f32[128]{0:T(128)S(1)} %convert_element_type.19), kind=kOutput, calls=%fused_computation.6.clone.1 | convolution fusion | flops 1077936128 | bytes 29360640 | tf_op jit(solution)/shard_map/while/body/bij,bjf->bif/dot_general | solution.py:25
  105.7 38.2 %scatter_fusion = f32[64,128,256]{2,1,0:T(8,128)} fusion(f32[64,128,256]{2,1,0:T(8,128)} %get-tuple-element.146, s32[128]{0:T(128)S(1)} %fusion.15, f32[128,128,256]{2,1,0:T(8,128)} %convolution_multiply_fusion.2), kind=kCustom, calls=%fused_computation.5.clone.1 | custom fusion | flops 4194304 | bytes 50332160 | tf_op jit(solution)/shard_map/while/body/scatter-add | solution.py:29
  143.9 0.1 compare_select_fusion.4
  143.9 1.0 gather_fusion.4
  144.9 1.0 gather_fusion.2
  145.9 1.0 gather_fusion
  146.9 11.2 %gather_fusion.1 = bf16[128,128,128]{2,1,0:T(8,128)(2,1)} fusion(bf16[768,128,128]{2,1,0:T(8,128)(2,1)} %get-tuple-element.163, s32[1024]{0:T(1024)S(1)} %pad_clamp_fusion.4), kind=kCustom, calls=%fused_computation.1.clone.1 | custom fusion | bytes 8389120 | tf_op jit(solution)/shard_map/while/body/gather | solution.py:39
  158.1 9.9 %gather_fusion.3 = bf16[128,128,256]{2,1,0:T(8,128)(2,1)} fusion(bf16[128,128,256]{2,1,0:T(8,128)(2,1)} %get-tuple-element.165, s32[1024]{0:T(1024)S(1)} %pad_clamp_fusion.5), kind=kCustom, calls=%fused_computation.3.clone.1 | custom fusion | bytes 16777728 | tf_op jit(solution)/shard_map/while/body/gather | solution.py:24
  168.0 12.7 %convolution_multiply_fusion.2 = f32[128,128,256]{2,1,0:T(8,128)} fusion(bf16[128,128,128]{2,1,0:T(8,128)(2,1)} %gather_fusion.1, bf16[128,128,256]{2,1,0:T(8,128)(2,1)} %gather_fusion.3, f32[128]{0:T(128)S(1)} %convert_element_type.19), kind=kOutput, calls=%fused_computation.6.clone.1 | convolution fusion | flops 1077936128 | bytes 29360640 | tf_op jit(solution)/shard_map/while/body/bij,bjf->bif/dot_general | solution.py:25
  180.7 38.1 %scatter_fusion = f32[64,128,256]{2,1,0:T(8,128)} fusion(f32[64,128,256]{2,1,0:T(8,128)} %get-tuple-element.146, s32[128]{0:T(128)S(1)} %fusion.15, f32[128,128,256]{2,1,0:T(8,128)} %convolution_multiply_fusion.2), kind=kCustom, calls=%fused_computation.5.clone.1 | custom fusion | flops 4194304 | bytes 50332160 | tf_op jit(solution)/shard_map/while/body/scatter-add | solution.py:29
  218.8 0.0 copy-start.1
  218.8 0.0 reduce-scatter.2.cloned.1.call-update
  218.9 221.3 %reduce-scatter.2.cloned.1.call-done = f32[2048,256]{1,0:T(8,128)} async-done(((f32[8192,256]{1,0:T(8,128)}), f32[2048,256]{1,0:T(8,128)}) %reduce-scatter.2.cloned.1.call-update) | async-done | bytes 2097168 | tf_op jit(solution)/shard_map/reduce_scatter | solution.py:47
  440.1 0.0 copy-done
  440.1 0.0 copy-done.1
  440.1 3.0 fusion.3
  (12 shorter events, 0.1 us)
Async XLA Ops:
  6.5 433.6 %copy-start = (bf16[256,256]{1,0:T(8,128)(2,1)S(1)}, bf16[256,256]{1,0:T(8,128)(2,1)}, u32[]{:S(2)}) copy-start(bf16[256,256]{1,0:T(8,128)(2,1)} %param.14) | copy-start | bytes 393220
  6.5 58.0 %all-gather.2.cloned.1.call-start = ((), (), s32[]{:S(2)}) async-start(), calls=%async_computation.1 | async-start | bytes 9437184 | tf_op jit(solution)/shard_map/all_gather | solution.py:15
  7.3 432.9 %reduce-scatter.2.cloned.1.call-start = ((), (), s32[]{:S(2)}) async-start(), calls=%async_computation.2 | async-start | bytes 10485760 | tf_op jit(solution)/shard_map/reduce_scatter | solution.py:47
  218.8 221.3 %copy-start.1 = (f32[256]{0:T(256)S(1)}, f32[256]{0:T(256)}, u32[]{:S(2)}) copy-start(f32[256]{0:T(256)} %param.15) | copy-start | bytes 3076
Sparse Core Ops, SparseCore 0:
  9.2 55.3 all-gather.1
  219.0 221.0 reduce-scatter.1
where the time goes:
time: 452 us; the launch traced here: 450 us
  waiting for transfers between devices  271 us (60%)
  other arithmetic  83.6 us (18%)
  local copies, waits for them, and re-layouts  52.2 us (12%)
  matrix products  28.4 us (6%)
  between operations  14.1 us (3%)
    reduce_scatter x1, waiting for transfers between devices, on_device(): lax.psum_scatter(partial_rows, 'col', scatter_dimension=0, tiled=True)  221 us
    scatter-add x2, other arithmetic, add_block(): return partial_sum.at[row_block].add(products)  76.3 us
    all_gather x1, waiting for transfers between devices, on_device(): panel = lax.all_gather(features, 'row', axis=0, tiled=True)  49.5 us
    dot_general x2, matrix products, add_block(): jnp.einsum('bij,bjf->bif', tile_block, chosen, preferred_element_type=jnp...  25.4 us
    gather x2, local copies, waits for them, and re-layouts, loop_step(): cell_tiles[picked]  22.3 us
    gather x2, local copies, waits for them, and re-layouts, add_block(): chosen = panel_tiles[col_block]  19.9 us
  transfers between devices with their start and end apart: 2, of which 2 were waited for; matrix products, arithmetic and copies ran while one was open for 2% of the time, Pallas kernels for 0%

commit v1 on v0

v1 whole, which is shorter than its diff:
```python
import functools

import jax
import jax.numpy as jnp
from jax import lax
from jax.experimental import pallas as pl
from jax.experimental.pallas import tpu as pltpu
from jax.sharding import PartitionSpec as P

SLOTS = 32
UNROLL = 8


def spmm_kernel(valid, rows, cols, panel_hbm, tiles_hbm, out_ref,
                slot_list, row_list, col_list, panel, total, ring, ring_sem, panel_sem):
    slot_count = valid.shape[0]
    row_tiles = out_ref.shape[0]
    panel_copy = pltpu.make_async_copy(panel_hbm, panel, panel_sem)
    panel_copy.start()

    def scan(step, count):
        for k in range(UNROLL):
            slot = step * UNROLL + k
            slot_list[count] = slot
            row_list[count] = rows[slot]
            col_list[count] = cols[slot]
            count = count + valid[slot]
        return count

    count = lax.fori_loop(0, slot_count // UNROLL, scan, jnp.int32(0))
    for k in range(UNROLL):
        slot_list[count + k] = 0
        row_list[count + k] = row_tiles
        col_list[count + k] = 0
    steps = (count + UNROLL - 1) // UNROLL
    filled = steps * UNROLL

    def fetch(index):
        place = lax.rem(index, SLOTS)
        return pltpu.make_async_copy(
            tiles_hbm.at[slot_list[index]], ring.at[place], ring_sem.at[place])

    def prime(index, carry):
        @pl.when(index < filled)
        def _():
            fetch(index).start()
        return carry

    lax.fori_loop(0, SLOTS, prime, 0)
    total[...] = jnp.zeros_like(total)
    panel_copy.wait()

    def step_body(step, carry):
        base = step * UNROLL
        for k in range(UNROLL):
            fetch(base + k).wait()
        for k in range(UNROLL):
            index = base + k
            product = jnp.dot(ring[lax.rem(index, SLOTS)], panel[col_list[index]],
                              preferred_element_type=jnp.float32)
            row = row_list[index]
            total[row] = total[row] + product
        for k in range(UNROLL):
            later = base + SLOTS + k

            @pl.when(later < filled)
            def _():
                fetch(later).start()
        return carry

    lax.fori_loop(0, steps, step_body, 0)

    def put(row, carry):
        out_ref[row] = total[row].astype(out_ref.dtype)
        return carry

    lax.fori_loop(0, row_tiles, put, 0)


def spmm(valid, rows, cols, panel, tiles, row_tiles):
    slot_count, tile_size = tiles.shape[0], tiles.shape[1]
    width = panel.shape[2]
    smem = pl.BlockSpec(memory_space=pltpu.SMEM)
    hbm = pl.BlockSpec(memory_space=pl.ANY)
    return pl.pallas_call(
        spmm_kernel,
        out_shape=jax.ShapeDtypeStruct((row_tiles, tile_size, width), jnp.bfloat16),
        in_specs=[smem, smem, smem, hbm, hbm],
        out_specs=pl.BlockSpec(memory_space=pltpu.VMEM),
        scratch_shapes=[
            pltpu.SMEM((slot_count + UNROLL,), jnp.int32),
            pltpu.SMEM((slot_count + UNROLL,), jnp.int32),
            pltpu.SMEM((slot_count + UNROLL,), jnp.int32),
            pltpu.VMEM(panel.shape, jnp.bfloat16),
            pltpu.VMEM((row_tiles + 1, tile_size, width), jnp.float32),
            pltpu.VMEM((SLOTS, tile_size, tile_size), jnp.bfloat16),
            pltpu.SemaphoreType.DMA((SLOTS,)),
            pltpu.SemaphoreType.DMA,
        ],
        compiler_params=pltpu.CompilerParams(vmem_limit_bytes=60 * 2**20),
        cost_estimate=pl.CostEstimate(
            flops=slot_count * tile_size * tile_size * width, bytes_accessed=32 * 2**20,
            transcendentals=0),
    )(valid, rows, cols, panel, tiles)


def on_device(features, tiles, tile_rows, tile_cols, valid, weight, bias):
    sub_rows, width = features.shape
    tile_size = tiles.shape[3]
    row_tiles = sub_rows * lax.axis_size("col") // tile_size
    panel = lax.all_gather(features, "row", axis=0, tiled=True).reshape(-1, tile_size, width)
    partial = spmm(valid[0, 0], tile_rows[0, 0], tile_cols[0, 0], panel, tiles[0, 0], row_tiles)
    summed = lax.psum_scatter(
        partial.reshape(row_tiles * tile_size, width), "col", scatter_dimension=0, tiled=True)
    mixed = jnp.dot(summed, weight, preferred_element_type=jnp.float32) + bias
    return jnp.maximum(mixed, 0.0).astype(jnp.bfloat16)


def solution(mesh):
    return jax.shard_map(
        on_device,
        mesh=mesh,
        in_specs=(
            P(("row", "col"), None),
            P("row", "col", None, None, None),
            P("row", "col", None),
            P("row", "col", None),
            P("row", "col", None),
            P(),
            P(),
        ),
        out_specs=P(("row", "col"), None),
        check_vma=False,
    )
```

time: 452 us -> 176 us (0.39)
  waiting for transfers between devices: 271 us -> 144 us
  other arithmetic: 83.6 us -> 3.86 us
  local copies, waits for them, and re-layouts: 52.2 us -> 0.01 us
  matrix products: 28.4 us -> 2.63 us
  Pallas kernels: 0 us -> 11.5 us
    reduce_scatter x1, waiting for transfers between devices: 221 us -> 89.5 us  [on_device(): lax.psum_scatter(partial.reshape(row_tiles * tile_size, width), 'col', sc...]
    scatter-add x2 -> x0, other arithmetic: 76.3 us -> none  [add_block(): return partial_sum.at[row_block].add(products)]
    gather x10 -> x0, local copies, waits for them, and re-layouts: 48 us -> none  [the longest x2 22.3 us: loop_step(): cell_tiles[picked]]
    dot_general x3 -> x1, matrix products: 28.4 us -> 2.63 us  [on_device(): mixed = jnp.dot(summed, weight, preferred_element_type=jnp.float32) + bias]
    pallas_call x0 -> x1, Pallas kernels: none -> 11.5 us  [spmm(): pl.pallas_call(spmm_kernel, out_shape=jax.ShapeDtypeStruct((row_tiles, ti...]
where the time goes in v1:
time: 176 us; the launch traced here: 175 us
  waiting for transfers between devices  144 us (82%)
  between operations  13.4 us (8%)
  Pallas kernels  11.5 us (7%)
  other arithmetic  3.86 us (2%)
  matrix products  2.63 us (1%)
    reduce_scatter x1, waiting for transfers between devices, on_device(): lax.psum_scatter(partial.reshape(row_tiles * tile_size, width), 'col', sc...  89.5 us
    all_gather x1, waiting for transfers between devices, on_device(): lax.all_gather(features, 'row', axis=0, tiled=True)  53.4 us
    pallas_call x1, Pallas kernels, spmm(): pl.pallas_call(spmm_kernel, out_shape=jax.ShapeDtypeStruct((row_tiles, ti...  11.5 us
    unnamed x3, other arithmetic  3.86 us
  transfers between devices with their start and end apart: 2, of which 2 were waited for; matrix products, arithmetic and copies ran while one was open for 2% of the time, Pallas kernels for 0%

profile of v1, /device:TPU:16, one launch (start us, length us, event | category | flops | bytes accessed | tf_op | source)
XLA Modules:
  0.0 175.0 jit_solution(15178974377993143339)
XLA Ops:
  6.5 0.0 copy-start
  6.5 0.0 all-gather.2.cloned.1.call-start
  6.5 0.7 all-gather.2.cloned.1.call-update
  7.3 0.0 reduce-scatter.2.cloned.1.call-start
  7.3 1.3 reduce.1.rows
  8.6 1.3 reduce.2.cols
  9.9 1.3 reduce.valid
  11.2 53.4 %all-gather.2.cloned.1.call-done = bf16[16384,256]{1,0:T(8,128)(2,1)} async-done(((bf16[2048,256]{1,0:T(8,128)(2,1)}), bf16[16384,256]{1,0:T(8,128)(2,1)}) %all-gather.2.cloned.1.call-update) | async-done | bytes 8388624 | tf_op jit(solution)/shard_map/all_gather | solution.py:111
  64.6 11.5 %shard_map.73 = bf16[64,128,256]{2,1,0:T(8,128)(2,1)} custom-call(s32[768]{0:T(1024)} %reduce.valid, s32[768]{0:T(1024)} %reduce.1.rows, s32[768]{0:T(1024)} %reduce.2.cols, bf16[128,128,256]{2,1,0:T(8,128)(2,1)} %bitcast.7, bf16[768,128,128]{2,1,0:T(8,128)(2,1)} %bitcast.5), custom_call_target="tpu_custom_call" | custom-call | flops 3221225472 | bytes 33554432 | tf_op jit(solution)/shard_map/pallas_call | solution.py:85
  76.1 0.0 copy-start.1
  76.1 0.0 reduce-scatter.2.cloned.1.call-update
  76.1 89.5 %reduce-scatter.2.cloned.1.call-done = bf16[2048,256]{1,0:T(8,128)(2,1)} async-done(((bf16[8192,256]{1,0:T(8,128)(2,1)}), bf16[2048,256]{1,0:T(8,128)(2,1)}) %reduce-scatter.2.cloned.1.call-update) | async-done | bytes 1048592 | tf_op jit(solution)/shard_map/reduce_scatter | solution.py:113
  165.6 0.0 copy-done
  165.6 0.0 copy-done.1
  165.6 2.6 %fusion.1 = bf16[2048,256]{1,0:T(8,128)(2,1)} fusion(bf16[2048,256]{1,0:T(8,128)(2,1)} %reduce-scatter.2.cloned.1.call-done, bf16[256,256]{1,0:T(8,128)(2,1)S(1)} %copy-done, f32[256]{0:T(256)S(1)} %copy-done.1), kind=kOutput, calls=%fused_computation.2 | convolution fusion | flops 270008320 | bytes 2229248 | tf_op jit(solution)/shard_map/dot_general | solution.py:115
Async XLA Ops:
  6.5 159.0 %copy-start = (bf16[256,256]{1,0:T(8,128)(2,1)S(1)}, bf16[256,256]{1,0:T(8,128)(2,1)}, u32[]{:S(2)}) copy-start(bf16[256,256]{1,0:T(8,128)(2,1)} %param.12) | copy-start | bytes 393220
  6.5 58.0 %all-gather.2.cloned.1.call-start = ((), (), s32[]{:S(2)}) async-start(), calls=%async_computation.1 | async-start | bytes 9437184 | tf_op jit(solution)/shard_map/all_gather | solution.py:111
  7.3 158.3 %reduce-scatter.2.cloned.1.call-start = ((), (), s32[]{:S(2)}) async-start(), calls=%async_computation.2 | async-start | bytes 5242880 | tf_op jit(solution)/shard_map/reduce_scatter | solution.py:113
  76.1 89.5 %copy-start.1 = (f32[256]{0:T(256)S(1)}, f32[256]{0:T(256)}, u32[]{:S(2)}) copy-start(f32[256]{0:T(256)} %param.13) | copy-start | bytes 3076
Sparse Core Ops, SparseCore 0:
  9.2 55.3 all-gather.1
  76.2 89.3 reduce-scatter.1

commit v2 on v1

--- a/solution.py
+++ b/solution.py
@@ -11,10 +11,10 @@
 UNROLL = 8
 
 
-def spmm_kernel(valid, rows, cols, panel_hbm, tiles_hbm, out_ref,
-                slot_list, row_list, col_list, panel, total, ring, ring_sem, panel_sem):
-    slot_count = valid.shape[0]
-    row_tiles = out_ref.shape[0]
+def spmm_kernel(valid, rows, cols, panel_hbm, tiles_hbm, total,
+                slot_list, row_list, col_list, panel, ring, ring_sem, panel_sem):
+    slot_count = valid.shape[2]
+    row_tiles = total.shape[0] - 1
     panel_copy = pltpu.make_async_copy(panel_hbm, panel, panel_sem)
     panel_copy.start()
 
@@ -22,9 +22,9 @@
         for k in range(UNROLL):
             slot = step * UNROLL + k
             slot_list[count] = slot
-            row_list[count] = rows[slot]
-            col_list[count] = cols[slot]
-            count = count + valid[slot]
+            row_list[count] = rows[0, 0, slot]
+            col_list[count] = cols[0, 0, slot]
+            count = count + valid[0, 0, slot]
         return count
 
     count = lax.fori_loop(0, slot_count // UNROLL, scan, jnp.int32(0))
@@ -38,7 +38,7 @@
     def fetch(index):
         place = lax.rem(index, SLOTS)
         return pltpu.make_async_copy(
-            tiles_hbm.at[slot_list[index]], ring.at[place], ring_sem.at[place])
+            tiles_hbm.at[0, 0, slot_list[index]], ring.at[place], ring_sem.at[place])
 
     def prime(index, carry):
         @pl.when(index < filled)
@@ -70,21 +70,15 @@
 
     lax.fori_loop(0, steps, step_body, 0)
 
-    def put(row, carry):
-        out_ref[row] = total[row].astype(out_ref.dtype)
-        return carry
-
-    lax.fori_loop(0, row_tiles, put, 0)
-
 
 def spmm(valid, rows, cols, panel, tiles, row_tiles):
-    slot_count, tile_size = tiles.shape[0], tiles.shape[1]
+    slot_count, tile_size = tiles.shape[2], tiles.shape[3]
     width = panel.shape[2]
     smem = pl.BlockSpec(memory_space=pltpu.SMEM)
     hbm = pl.BlockSpec(memory_space=pl.ANY)
     return pl.pallas_call(
         spmm_kernel,
-        out_shape=jax.ShapeDtypeStruct((row_tiles, tile_size, width), jnp.bfloat16),
+        out_shape=jax.ShapeDtypeStruct((row_tiles + 1, tile_size, width), jnp.float32),
         in_specs=[smem, smem, smem, hbm, hbm],
         out_specs=pl.BlockSpec(memory_space=pltpu.VMEM),
         scratch_shapes=[
@@ -92,7 +86,6 @@
             pltpu.SMEM((slot_count + UNROLL,), jnp.int32),
             pltpu.SMEM((slot_count + UNROLL,), jnp.int32),
             pltpu.VMEM(panel.shape, jnp.bfloat16),
-            pltpu.VMEM((row_tiles + 1, tile_size, width), jnp.float32),
             pltpu.VMEM((SLOTS, tile_size, tile_size), jnp.bfloat16),
             pltpu.SemaphoreType.DMA((SLOTS,)),
             pltpu.SemaphoreType.DMA,
@@ -104,15 +97,264 @@
     )(valid, rows, cols, panel, tiles)
 
 
+MESH = pl.DeviceIdType.MESH
+PIECES = 2
+
+
+def gather_steps(features, lane, panel, send_sem, recv_sem, local_sem, rows):
+    sub_rows, width = panel.shape[1], panel.shape[2]
+    cut = sub_rows // 2
+    me = lax.axis_index("row")
+    chips = rows // 2
+    core, chip = lax.rem(me, 2), me // 2
+    partner = chip * 2 + (1 - core)
+    own = features.at[:, pl.ds(lane * width, width)]
+
+    def half(ref, k):
+        return ref.at[pl.ds(k * cut, cut)]
+
+    def copy(src, block, k, number, target):
+        return pltpu.make_async_remote_copy(
+            src_ref=src, dst_ref=half(panel.at[block], k), send_sem=send_sem.at[number],
+            recv_sem=recv_sem.at[number], device_id={"row": target}, device_id_type=MESH)
+
+    def held(block, k):
+        return half(panel.at[block], k)
+
+    if chips == 4:
+        over_x, over_y = lax.rem(chip, 2), chip // 2
+        x_side = (over_y * 2 + (1 - over_x)) * 2 + core
+        y_side = ((1 - over_y) * 2 + over_x) * 2 + core
+        across = ((1 - over_y) * 2 + (1 - over_x)) * 2 + core
+        peers = [x_side, y_side]
+        sources = [x_side, y_side, y_side, x_side]
+        own_copies = [copy(half(own, 0), me, 0, 0, x_side), copy(half(own, 1), me, 1, 1, y_side),
+                      copy(half(own, 1), me, 1, 2, x_side), copy(half(own, 0), me, 0, 3, y_side)]
+        passed = {0: copy(held(x_side, 0), x_side, 0, 4, y_side),
+                  1: copy(held(y_side, 1), y_side, 1, 5, x_side)}
+        arriving = [(x_side, 0), (y_side, 1), (x_side, 1), (y_side, 0), (across, 0), (across, 1)]
+    else:
+        peers = [lax.rem(chip + k, chips) * 2 + core for k in range(1, chips)]
+        from_peers = [lax.rem(chip + chips - k, chips) * 2 + core for k in range(1, chips)]
+        own_copies, passed, arriving = [], {}, []
+        for place, (peer, giver) in enumerate(zip(peers, from_peers)):
+            for k in range(2):
+                own_copies.append(copy(half(own, k), me, k, 2 * place + k, peer))
+                arriving.append((giver, k))
+    direct = len(arriving)
+    started = list(own_copies)
+    keep = pltpu.make_async_copy(own, panel.at[me], local_sem)
+
+    def begin():
+        for item in own_copies:
+            item.start()
+        for k in range(2):
+            item = copy(half(own, k), me, k, direct + k, partner)
+            item.start()
+            started.append(item)
+        keep.start()
+
+    def receive(number):
+        block, k = arriving[number]
+        copy(held(block, k), block, k, number, partner).wait_recv()
+        if number in passed:
+            passed[number].start()
+            started.append(passed[number])
+        item = copy(held(block, k), block, k, direct + 2 + number, partner)
+        item.start()
+        started.append(item)
+
+    def finish():
+        for number in range(direct + 2):
+            copy(held(me, 0), me, 0, direct + number, partner).wait_recv()
+        for item in started:
+            item.wait_send()
+        keep.wait()
+
+    steps = [functools.partial(receive, number) for number in range(direct)]
+    return peers + [partner], begin, steps, finish
+
+
+def reduce_steps(partial, summed, to_right, to_left, from_left, from_right, total, sems, columns):
+    tiles_each = summed.shape[0]
+    cut = tiles_each // PIECES
+    me = lax.axis_index("col")
+    right_send, right_recv, left_send, left_recv = sems
+
+    def move(rightward, dest, piece):
+        place = dest - 1 if rightward else dest
+        outbox, inbox = (to_right, from_left) if rightward else (to_left, from_right)
+        send, recv = (right_send, right_recv) if rightward else (left_send, left_recv)
+        part = pl.ds(piece * cut, cut)
+        inner = (me < dest) if rightward else (me > dest)
+        first = (me == 0) if rightward else (me == columns - 1)
+        number = place * PIECES + piece
+        target = me + 1 if rightward else me - 1
+        item = pltpu.make_async_remote_copy(
+            src_ref=outbox.at[place, part], dst_ref=inbox.at[place, part],
+            send_sem=send.at[number], recv_sem=recv.at[number],
+            device_id={"col": target}, device_id_type=MESH)
+        here = pl.ds(dest * tiles_each + piece * cut, cut)
+
+        def open_chain():
+            @pl.when(first)
+            def _():
+                outbox[place, part] = partial[here].astype(outbox.dtype)
+                item.start()
+
+        def pass_on():
+            @pl.when(jnp.logical_and(inner, jnp.logical_not(first)))
+            def _():
+                item.wait_recv()
+                outbox[place, part] = (
+                    partial[here] + inbox[place, part].astype(jnp.float32)).astype(outbox.dtype)
+                item.start()
+
+        def close_chain():
+            @pl.when(me == dest)
+            def _():
+                item.wait_recv()
+                total[part] = total[part] + inbox[place, part].astype(jnp.float32)
+
+        def drain():
+            @pl.when(inner)
+            def _():
+                item.wait_send()
+
+        return open_chain, pass_on, close_chain, drain
+
+    links = []
+    for turn in range(columns - 1):
+        for piece in range(PIECES):
+            links.append(move(True, columns - 1 - turn, piece))
+            links.append(move(False, turn, piece))
+
+    def begin():
+        for link in links:
+            link[0]()
+        total[...] = partial[pl.ds(me * tiles_each, tiles_each)]
+
+    def finish():
+        for link in links:
+            link[2]()
+        summed[...] = total[...].astype(summed.dtype)
+        for link in links:
+            link[3]()
+
+    return begin, [link[1] for link in links], finish
+
+
+def exchange_kernel(gathering, reducing, lane, rows, columns, *refs):
+    refs = list(refs)
+    features = refs.pop(0) if gathering else None
+    partial = refs.pop(0) if reducing else None
+    panel = refs.pop(0) if gathering else None
+    summed = refs.pop(0) if reducing else None
+    peers, queue = [], []
+    if gathering:
+        send_sem, recv_sem, local_sem = refs.pop(0), refs.pop(0), refs.pop(0)
+        peers, gather_begin, gather_list, gather_finish = gather_steps(
+            features, lane, panel, send_sem, recv_sem, local_sem, rows)
+    if reducing:
+        reduce_begin, reduce_list, reduce_finish = reduce_steps(
+            partial, summed, *refs[:5], refs[5:9], columns)
+
+    barrier = pltpu.get_barrier_semaphore()
+    for peer in peers:
+        pl.semaphore_signal(barrier, inc=1, device_id={"row": peer}, device_id_type=MESH)
+    expected = len(peers)
+    if reducing:
+        me = lax.axis_index("col")
+
+        @pl.when(me > 0)
+        def _():
+            pl.semaphore_signal(barrier, inc=1, device_id={"col": me - 1}, device_id_type=MESH)
+
+        @pl.when(me < columns - 1)
+        def _():
+            pl.semaphore_signal(barrier, inc=1, device_id={"col": me + 1}, device_id_type=MESH)
+
+        inside = jnp.logical_and(me > 0, me < columns - 1)
+
+        @pl.when(inside)
+        def _():
+            pl.semaphore_wait(barrier, expected + 2)
+
+        @pl.when(jnp.logical_not(inside))
+        def _():
+            pl.semaphore_wait(barrier, expected + 1)
+    else:
+        pl.semaphore_wait(barrier, expected)
+
+    if gathering:
+        gather_begin()
+    if reducing:
+        reduce_begin()
+    gather_queue = list(gather_list) if gathering else []
+    reduce_queue = list(reduce_list) if reducing else []
+    while gather_queue or reduce_queue:
+        for queue in (gather_queue, reduce_queue):
+            for _ in range(2):
+                if queue:
+                    queue.pop(0)()
+    if gathering:
+        gather_finish()
+    if reducing:
+        reduce_finish()
+
+
+def exchange(number, features, lane, partial, width, tile_size, rows, columns):
+    gathering, reducing = features is not None, partial is not None
+    hbm, vmem = pl.BlockSpec(memory_space=pl.ANY), pl.BlockSpec(memory_space=pltpu.VMEM)
+    operands, in_specs, out_shape, out_specs, scratch = [], [], [], [], []
+    if gathering:
+        sub_rows = features.shape[0]
+        operands.append(features)
+        in_specs.append(hbm)
+        out_shape.append(jax.ShapeDtypeStruct((rows, sub_rows, width), jnp.bfloat16))
+        out_specs.append(hbm)
+        chips = rows // 2
+        copies = 2 * (6 if chips == 4 else 2 * (chips - 1)) + 2
+        scratch += [pltpu.SemaphoreType.DMA((copies,)), pltpu.SemaphoreType.DMA((copies,)),
+                    pltpu.SemaphoreType.DMA]
+    if reducing:
+        tiles_each = (partial.shape[0] - 1) // columns
+        operands.append(partial)
+        in_specs.append(vmem)
+        out_shape.append(jax.ShapeDtypeStruct((tiles_each, tile_size, width), jnp.bfloat16))
+        out_specs.append(vmem)
+        scratch += [pltpu.VMEM((columns - 1, tiles_each, tile_size, width), jnp.bfloat16)] * 4
+        scratch += [pltpu.VMEM((tiles_each, tile_size, width), jnp.float32)]
+        scratch += [pltpu.SemaphoreType.DMA(((columns - 1) * PIECES,))] * 4
+    return pl.pallas_call(
+        functools.partial(exchange_kernel, gathering, reducing, lane, rows, columns),
+        out_shape=out_shape, in_specs=in_specs, out_specs=out_specs, scratch_shapes=scratch,
+        compiler_params=pltpu.CompilerParams(
+            collective_id=number, has_side_effects=True, vmem_limit_bytes=60 * 2**20),
+    )(*operands)
+
+
 def on_device(features, tiles, tile_rows, tile_cols, valid, weight, bias):
-    sub_rows, width = features.shape
+    sub_rows, channels = features.shape
     tile_size = tiles.shape[3]
-    row_tiles = sub_rows * lax.axis_size("col") // tile_size
-    panel = lax.all_gather(features, "row", axis=0, tiled=True).reshape(-1, tile_size, width)
-    partial = spmm(valid[0, 0], tile_rows[0, 0], tile_cols[0, 0], panel, tiles[0, 0], row_tiles)
-    summed = lax.psum_scatter(
-        partial.reshape(row_tiles * tile_size, width), "col", scatter_dimension=0, tiled=True)
-    mixed = jnp.dot(summed, weight, preferred_element_type=jnp.float32) + bias
+    rows, columns = lax.axis_size("row"), lax.axis_size("col")
+    row_tiles = sub_rows * columns // tile_size
+    width = min(channels, 128)
+    lanes = channels // width
+    cells = (valid, tile_rows, tile_cols)
+    sums, partial = [], None
+    for lane in range(lanes + 1):
+        results = list(exchange(
+            lane, features if lane < lanes else None, lane, partial, width, tile_size, rows, columns))
+        if partial is not None:
+            sums.append(results.pop().reshape(sub_rows, width))
+        if lane < lanes:
+            panel = results[0].reshape(-1, tile_size, width)
+            partial = spmm(*cells, panel, tiles, row_tiles)
+    mixed = bias
+    for lane in range(lanes):
+        mixed = mixed + jnp.dot(sums[lane], weight[lane * width:(lane + 1) * width],
+                                preferred_element_type=jnp.float32)
     return jnp.maximum(mixed, 0.0).astype(jnp.bfloat16)
 
 

time: 176 us -> 160 us (0.909)
  Pallas kernels: 11.5 us -> 157 us
  waiting for transfers between devices: 144 us -> 0 us
  between operations: 13.4 us -> 0.1 us
  other arithmetic: 3.86 us -> 0 us
    pallas_call x1 -> x5, Pallas kernels: 11.5 us -> 157 us  [the longest x3 118 us: exchange(): pl.pallas_call(functools.partial(exchange_kernel, gathering, reducing, la...]
    reduce_scatter x1 -> x0, waiting for transfers between devices: 89.5 us -> none  [on_device(): lax.psum_scatter(partial.reshape(row_tiles * tile_size, width), 'col', sc...]
    all_gather x1 -> x0, waiting for transfers between devices: 53.4 us -> none  [on_device(): lax.all_gather(features, 'row', axis=0, tiled=True)]
    unnamed x3 -> x0, other arithmetic: 3.86 us -> none
  transfers between devices with their start and end apart: 2 -> 0, of which waited for: 2 -> 0; matrix products, arithmetic and copies ran while one was open for 2% -> 0% of each run, Pallas kernels for 0% -> 0%
where the time goes in v2:
time: 160 us; the launch traced here: 159 us
  Pallas kernels  157 us (98%)
  matrix products  1.8 us (1%)
    pallas_call x3, Pallas kernels, exchange(): pl.pallas_call(functools.partial(exchange_kernel, gathering, reducing, la...  118 us
    pallas_call x2, Pallas kernels, spmm(): pl.pallas_call(spmm_kernel, out_shape=jax.ShapeDtypeStruct((row_tiles + 1...  39.1 us

profile of v2, /device:TPU:16, one launch (start us, length us, event | category | flops | bytes accessed | tf_op | source)
XLA Modules:
  0.0 159.3 jit_solution(11556524302493960632)
XLA Ops:
  0.0 22.7 %shard_map.73 = bf16[8,2048,128]{2,1,0:T(8,128)(2,1)} custom-call(bf16[2048,256]{1,0:T(8,128)(2,1)} %refs_0_.3), custom_call_target="tpu_custom_call" | custom-call | tf_op jit(solution)/shard_map/pallas_call | solution.py:329
  22.7 19.6 %shard_map.74.refs_1_ = f32[65,128,128]{2,1,0:T(8,128)} custom-call(s32[1,1,768]{2,1,0:T(1,128)} %valid.3, s32[1,1,768]{2,1,0:T(1,128)} %rows.3, s32[1,1,768]{2,1,0:T(1,128)} %cols.3, bf16[128,128,128]{2,1,0:T(8,128)(2,1)} %bitcast.6, bf16[1,1,768,128,128]{4,3,2,1,0:T(8,128)(2,1)} %tiles_hbm.3), custom_call_target="tpu_custom_call" | custom-call | flops 1610612736 | bytes 33554432 | tf_op jit(solution)/shard_map/pallas_call | solution.py:79
  42.3 48.2 %shard_map.75 = (bf16[8,2048,128]{2,1,0:T(8,128)(2,1)}, bf16[16,128,128]{2,1,0:T(8,128)(2,1)}) custom-call(bf16[2048,256]{1,0:T(8,128)(2,1)} %refs_0_.3, f32[65,128,128]{2,1,0:T(8,128)} %shard_map.74.refs_1_), custom_call_target="tpu_custom_call" | custom-call | tf_op jit(solution)/shard_map/pallas_call | solution.py:329
  90.4 19.5 %shard_map.76.refs_0_ = f32[65,128,128]{2,1,0:T(8,128)} custom-call(s32[1,1,768]{2,1,0:T(1,128)} %valid.3, s32[1,1,768]{2,1,0:T(1,128)} %rows.3, s32[1,1,768]{2,1,0:T(1,128)} %cols.3, bf16[128,128,128]{2,1,0:T(8,128)(2,1)} %bitcast.7, bf16[1,1,768,128,128]{4,3,2,1,0:T(8,128)(2,1)} %tiles_hbm.3), custom_call_target="tpu_custom_call" | custom-call | flops 1610612736 | bytes 33554432 | tf_op jit(solution)/shard_map/pallas_call | solution.py:79
  110.0 0.0 copy-start.1
  110.0 0.0 copy-start.2
  110.0 0.0 copy-start.3
  110.0 46.8 %shard_map.77 = bf16[16,128,128]{2,1,0:T(8,128)(2,1)} custom-call(f32[65,128,128]{2,1,0:T(8,128)} %shard_map.76.refs_0_), custom_call_target="tpu_custom_call" | custom-call | tf_op jit(solution)/shard_map/pallas_call | solution.py:329
  156.9 0.0 copy-start
  156.9 0.0 copy-done.1
  156.9 0.0 copy-done.2
  156.9 0.0 copy-done.3
  156.9 0.4 convolution_add_fusion.1
  157.3 0.6 copy-done
  157.9 1.4 fusion.1
Async XLA Ops:
  110.0 46.9 %copy-start.1 = (bf16[16,128,128]{2,1,0:T(8,128)(2,1)S(1)}, bf16[16,128,128]{2,1,0:T(8,128)(2,1)}, u32[]{:S(2)}) copy-start(bf16[16,128,128]{2,1,0:T(8,128)(2,1)} %get-tuple-element.7) | copy-start | bytes 1572868
  110.0 46.9 %copy-start.2 = (bf16[256,256]{1,0:T(8,128)(2,1)S(1)}, bf16[256,256]{1,0:T(8,128)(2,1)}, u32[]{:S(2)}) copy-start(bf16[256,256]{1,0:T(8,128)(2,1)} %param.12) | copy-start | bytes 393220
  110.0 46.9 %copy-start.3 = (f32[256]{0:T(256)S(1)}, f32[256]{0:T(256)}, u32[]{:S(2)}) copy-start(f32[256]{0:T(256)} %param.13) | copy-start | bytes 3076
  156.9 1.0 copy-start
